TPU v7x, 32 devices: a whole 2x2x4 slice. The times are simulated.
32 devices in a mesh: tok: 8 (over y, x, core), exp: 4 (over z).
Axes of the slice: x: 2, y: 2, z: 4, core: 2. Of those that a mesh axis runs over, the one named last changes fastest.
Arguments:
- expert_rows: bfloat16 [4, 2048, 4096], P('exp', 'tok'), may hold values from -480 to 480
- router_input: bfloat16 [2048, 4096], P(('tok', 'exp')), may hold values from -6 to 6
- router_weight: float32 [4096, 4], replicated, may hold values from -0.09375 to 0.09375
- assign: int32 [2048, 2], P(('tok', 'exp')), may hold values from 0 to 3, all different within a row
- targets: int32 [2048], P(('tok', 'exp')), may hold values from 0 to 15999
- head: bfloat16 [4096, 16000], P('tok', 'exp'), may hold values from -0.35 to 0.35
Outputs:
- token_loss: float32 [2048], P(('tok', 'exp'))
- router_grad: float32 [4096, 4], replicated
- mean_loss: float32 [], replicated
All inputs are finite; a program needn't handle non-finite values.
Results may differ from a plain program's by a relative error of at most 0.007.
Values may be sent and summed in bfloat16 or wider, within the bound.
A program may use at most 128 MiB of HBM per device.

v0:
```python
import math
import jax
import jax.numpy as jnp
from jax import lax
from jax.sharding import PartitionSpec as P


def shards(expert_rows, router_input, router_weight, assign, targets, head):
    experts = router_weight.shape[1]
    own_rows = router_input.shape[0]
    tokens_all = own_rows * lax.axis_size("tok") * lax.axis_size("exp")
    loss_scale = 1.0 / math.sqrt(tokens_all)
    inputs = router_input.astype(jnp.float32)
    gate_logits = jnp.dot(inputs, router_weight, precision=lax.Precision.HIGHEST)
    labels = jnp.arange(experts, dtype=jnp.int32)
    first_hot = (assign[:, 0:1] == labels[None, :]).astype(jnp.float32)
    second_hot = (assign[:, 1:2] == labels[None, :]).astype(jnp.float32)
    differ = first_hot - second_hot
    mix_share = jax.nn.sigmoid(jnp.sum(gate_logits * differ, axis=1))
    mixing = mix_share[:, None] * first_hot + (1.0 - mix_share)[:, None] * second_hot
    local_rows = lax.all_to_all(expert_rows, "exp", split_axis=1, concat_axis=0, tiled=True)
    local_wide = local_rows.astype(jnp.float32)
    mixed_own = jnp.sum(mixing.T[:, :, None] * local_wide, axis=0).astype(jnp.bfloat16)
    mixed_rows, group_targets = (
        lax.all_gather(mixed_own, "exp", axis=0, tiled=True),
        lax.all_gather(targets, "exp", axis=0, tiled=True),
    )
    shard_width = head.shape[1]
    full_head = lax.all_gather(head, "tok", axis=0, tiled=True)
    logits = jnp.dot(mixed_rows, full_head, preferred_element_type=jnp.float32)
    first_col = lax.axis_index("exp") * shard_width
    columns = first_col + jnp.arange(shard_width, dtype=jnp.int32)
    target_hit = group_targets[:, None] == columns[None, :]
    picked = jnp.sum(jnp.where(target_hit, logits, 0.0), axis=1)
    local_top = jnp.max(logits, axis=1)
    row_top = lax.pmax(local_top, "exp")
    exp_total, target_logit = lax.psum(
        (jnp.sum(jnp.exp(logits - row_top[:, None]), axis=1), picked), "exp"
    )
    log_total = row_top + jnp.log(exp_total)
    group_loss = log_total - target_logit
    own_loss = lax.dynamic_slice_in_dim(group_loss, lax.axis_index("exp") * own_rows, own_rows, 0)
    loss_sum = lax.psum(jnp.sum(own_loss), ("tok", "exp"))
    slope = (
        loss_scale * (jnp.exp(logits - log_total[:, None]) - target_hit.astype(jnp.float32))
    ).astype(jnp.bfloat16)
    hidden_slope = lax.psum_scatter(
        lax.dot_general(
            slope, full_head, (((1,), (1,)), ((), ())), preferred_element_type=jnp.float32
        ).astype(jnp.bfloat16),
        "exp",
        scatter_dimension=0,
        tiled=True,
    ).astype(jnp.float32)
    weight_slope = jnp.sum(hidden_slope[None, :, :] * local_wide, axis=2).T
    spread = jnp.sum(weight_slope * differ, axis=1) * mix_share * (1.0 - mix_share)
    gate_slope = spread[:, None] * differ
    router_part = jnp.dot(inputs.T, gate_slope, precision=lax.Precision.HIGHEST)
    router_sum = lax.psum(router_part, ("tok", "exp"))
    mean_loss = loss_sum / tokens_all
    return (own_loss, router_sum, mean_loss)


def solution(mesh):
    in_specs = (
        P("exp", "tok", None),
        P(("tok", "exp"), None),
        P(),
        P(("tok", "exp"), None),
        P(("tok", "exp")),
        P("tok", "exp"),
    )
    out_specs = (P(("tok", "exp")), P(), P())
    return jax.shard_map(shards, mesh=mesh, in_specs=in_specs, out_specs=out_specs, check_vma=False)
```

profile of v0, /device:TPU:1, one launch (start us, length us, event | category | flops | bytes accessed | tf_op | source)
XLA Modules:
  0.0 542.0 jit_solution(5459968139769704115)
XLA Ops:
  7.2 0.0 copy-start
  7.2 8.4 %copy.16 = bf16[1,256,4096]{2,0,1:T(2,128)(2,1)} copy(bf16[1,256,4096]{2,1,0:T(8,128)(2,1)} %param.6) | data formatting | bytes 4194304 | tf_op args[0]
  15.6 0.5 broadcast.107
  16.1 13.5 %reduce.1 = bf16[256,4096]{1,0:T(8,128)(2,1)S(1)} reduce(bf16[256,1,4096]{2,1,0:T(2,128)(2,1)} %bitcast.29, bf16[]{:T(256)} %broadcast.107), dimensions={1}, to_apply=%bitcast.25.reduce_sub_computation | reduce | bytes 4194306
  29.6 0.0 copy-start.3
  29.6 0.0 copy-start.2
  29.6 2.8 reshape.110
  32.4 5.4 all-to-all-start
  37.8 0.0 all-gather.3.cloned.1.call-start
  37.8 0.0 copy-done.3
  37.8 0.0 copy-done
  37.8 0.0 copy-done.2
  37.9 0.5 fusion.10
  38.4 47.2 %all-to-all-done = bf16[4,2,131072]{2,1,0:T(2,128)(2,1)S(1)} async-done(((bf16[4,2,131072]{2,1,0:T(2,128)(2,1)}), bf16[4,2,131072]{2,1,0:T(2,128)(2,1)S(1)}, u32[]{:S(2)}, u32[]{:S(2)}) %all-to-all-start) | async-done | bytes 2097184 | tf_op jit(solution)/shard_map/all_to_all | solution.py:21
  85.6 3.3 reshape.111
  88.9 6.0 %copy_convert_fusion = f32[1,256,4096]{2,1,0:T(8,128)S(1)} fusion(bf16[1,256,4096]{2,0,1:T(2,128)(2,1)} %bitcast.27), kind=kLoop, calls=%fused_computation.12 | loop fusion | flops 1048576 | bytes 6291456 | tf_op jit(solution)/shard_map/convert_element_type | solution.py:22
  94.9 0.0 copy-start.5
  94.9 0.0 copy-start.4
  94.9 1.4 multiply_reduce_fusion
  96.3 0.0 all-gather.3.cloned.1.call-update
  96.3 0.0 all-gather.5.cloned.1.call-start
  96.3 0.7 all-gather.5.cloned.1.call-update
  97.1 0.2 reduce-scatter.2.cloned.1.call-start
  97.3 0.0 copy-done.5
  97.3 0.6 dynamic-slice
  98.5 0.0 copy-done.4
  98.6 0.2 dynamic-update-slice
  98.8 4.0 all-reduce
  102.8 39.0 %all-gather.3.cloned.1.call-done = bf16[256,4096]{1,0:T(8,128)(2,1)} async-done(((bf16[64,4096]{1,0:T(8,128)(2,1)}), bf16[256,4096]{1,0:T(8,128)(2,1)}) %all-gather.3.cloned.1.call-update) | async-done | bytes 2097168 | tf_op jit(solution)/shard_map/all_gather | solution.py:25
  141.8 165.1 %all-gather.5.cloned.1.call-done = bf16[4096,4000]{0,1:T(8,128)(2,1)} async-done(((bf16[512,4000]{0,1:T(8,128)(2,1)}), bf16[4096,4000]{0,1:T(8,128)(2,1)}) %all-gather.5.cloned.1.call-update) | async-done | bytes 32768016 | tf_op jit(solution)/shard_map/all_gather | solution.py:29
  306.9 16.2 %fusion.19 = (f32[256]{0:T(256)S(1)}, f32[256,4000]{0,1:T(8,128)}) fusion(bf16[256,4096]{1,0:T(8,128)(2,1)} %all-gather.3.cloned.1.call-done, bf16[4096,4000]{0,1:T(8,128)(2,1)} %all-gather.5.cloned.1.call-done), kind=kOutput, calls=%fused_computation.41 | convolution fusion | flops 8389632000 | bytes 38962176 | tf_op jit(solution)/shard_map/dot_general | solution.py:30
  323.2 9.7 %pmax.7 = f32[256]{0:T(256)S(1)} all-reduce(f32[256]{0:T(256)S(1)} %get-tuple-element.15), channel_id=1, replica_groups=mesh['tok'=8,'exp'=4] {'exp'}, use_global_device_ids=true, to_apply=%region_3.4 | all-reduce | flops 256 | bytes 2048 | tf_op jit(solution)/shard_map/pmax | solution.py:36
  332.8 3.9 fusion.1
  336.7 6.6 %all-reduce.1 = (f32[256]{0:T(256)S(1)}, f32[256]{0:T(256)S(1)}) all-reduce(f32[256]{0:T(256)S(1)} %get-tuple-element.4, f32[256]{0:T(256)S(1)} %get-tuple-element.3), channel_id=1, replica_groups=mesh['tok'=8,'exp'=4] {'exp'}, use_global_device_ids=true, to_apply=%region_5.6 | all-reduce | flops 512 | bytes 4096 | tf_op jit(solution)/shard_map/psum | solution.py:37
  343.3 17.2 %convolution_convert_fusion = bf16[256,4096]{1,0:T(8,128)(2,1)} fusion(bf16[4096,4000]{0,1:T(8,128)(2,1)} %all-gather.5.cloned.1.call-done, f32[256,4000]{0,1:T(8,128)} %get-tuple-element.16, f32[256]{0:T(256)S(1)} %get-tuple-element.10, s32[256]{0:T(256)S(1)} %all-reduce, s32[4000]{0:T(1024)S(1)} %iota_add_fusion), kind=kOutput, calls=%fused_computation | convolution fusion | flops 8395800576 | bytes 38979200 | tf_op jit(solution)/shard_map/dot_general | solution.py:48
  360.5 0.0 reduce-scatter.2.cloned.1.call-update
  360.5 0.0 all-reduce.4.cloned.1.call-start
  360.6 45.4 %reduce-scatter.2.cloned.1.call-done = bf16[64,4096]{1,0:T(8,128)(2,1)} async-done(((bf16[256,4096]{1,0:T(8,128)(2,1)}), bf16[64,4096]{1,0:T(8,128)(2,1)}) %reduce-scatter.2.cloned.1.call-update) | async-done | bytes 524304 | tf_op jit(solution)/shard_map/reduce_scatter | solution.py:47
  406.0 0.0 copy-start.1
  406.0 1.7 mul.89
  407.6 0.7 copy-done.1
  408.3 2.4 fusion
  410.7 0.1 reduce_sum.70
  410.8 1.0 convolution_bitcast_fusion
  411.8 0.0 all-reduce.4.cloned.1.call-update
  411.8 1.2 fusion.17
  413.0 39.8 %psum.31 = f32[]{:T(128)} all-reduce(f32[]{:T(128)} %get-tuple-element.7), channel_id=1, replica_groups=mesh['tok'=8,'exp'=4] {'tok','exp'}, use_global_device_ids=true, to_apply=%region_13.14 | all-reduce | flops 1 | bytes 8 | tf_op jit(solution)/shard_map/psum | solution.py:43
  453.4 79.5 %all-reduce.4.cloned.1.call-done = f32[4096,4]{0,1:T(4,128)} async-done(((f32[4096,4]{0,1:T(4,128)}), f32[4096,4]{0,1:T(4,128)}) %all-reduce.4.cloned.1.call-update) | async-done | bytes 65552 | tf_op jit(solution)/shard_map/psum | solution.py:59
  532.9 1.5 copy.19
  (8 shorter events, 0.1 us)
Async XLA Ops:
  7.2 30.7 %copy-start = (bf16[64,4096]{1,0:T(8,128)(2,1)S(1)}, bf16[64,4096]{1,0:T(8,128)(2,1)}, u32[]{:S(2)}) copy-start(bf16[64,4096]{1,0:T(8,128)(2,1)} %param.7) | copy-start | bytes 1572868
  29.6 8.2 %copy-start.3 = (s32[64,2]{0,1:T(2,128)S(1)}, s32[64,2]{0,1:T(2,128)}, u32[]{:S(2)}) copy-start(s32[64,2]{0,1:T(2,128)} %param.9) | copy-start | bytes 1540
  29.6 8.2 %copy-start.2 = (f32[4096,4]{0,1:T(4,128)S(1)}, f32[4096,4]{0,1:T(4,128)}, u32[]{:S(2)}) copy-start(f32[4096,4]{0,1:T(4,128)} %param.8) | copy-start | bytes 196612
  32.4 53.2 %all-to-all-start = ((bf16[4,2,131072]{2,1,0:T(2,128)(2,1)}), bf16[4,2,131072]{2,1,0:T(2,128)(2,1)S(1)}, u32[]{:S(2)}, u32[]{:S(2)}) async-start(bf16[4,2,131072]{2,1,0:T(2,128)(2,1)} %reshape.110), calls=%async_computation | async-start | bytes 4194304 | tf_op jit(solution)/shard_map/all_to_all | solution.py:21
  37.8 104.0 %all-gather.3.cloned.1.call-start = ((), (), s32[]{:S(2)}) async-start(), calls=%async_computation.2 | async-start | bytes 2621440 | tf_op jit(solution)/shard_map/all_gather | solution.py:25
  94.9 2.4 copy-start.5
  94.9 3.6 copy-start.4
  96.3 210.6 %all-gather.5.cloned.1.call-start = ((), (), s32[]{:S(2)}) async-start(), calls=%async_computation.3 | async-start | bytes 36864000 | tf_op jit(solution)/shard_map/all_gather | solution.py:29
  97.1 308.9 %reduce-scatter.2.cloned.1.call-start = ((), (), s32[]{:S(2)}) async-start(), calls=%async_computation.4 | async-start | bytes 2621440 | tf_op jit(solution)/shard_map/reduce_scatter | solution.py:47
  360.5 172.3 %all-reduce.4.cloned.1.call-start = ((), (), s32[]{:S(2)}) async-start(), calls=%async_computation.5 | async-start | bytes 131072 | tf_op jit(solution)/shard_map/psum | solution.py:59
  406.0 2.3 copy-start.1
Sparse Core Ops, SparseCore 0:
  96.4 45.3 all-gather.2
  143.6 163.2 all-gather.4
  360.7 45.2 reduce-scatter.1
  412.0 120.8 all-reduce.3
where the time goes:
time: 543 us; the launch traced here: 542 us
  waiting for transfers between devices  377 us (69%)
  blocking collectives  60.1 us (11%)
  matrix products  34.9 us (6%)
  other arithmetic  28.4 us (5%)
  local copies, waits for them, and re-layouts  19.7 us (4%)
  between operations  16.3 us (3%)
  starting transfers between devices  5.71 us (1%)
    all_gather x1, waiting for transfers between devices, shards(): full_head = lax.all_gather(head, 'tok', axis=0, tiled=True)  165 us
    psum x1, waiting for transfers between devices, shards(): router_sum = lax.psum(router_part, ('tok', 'exp'))  79.5 us
    all_to_all x1, waiting for transfers between devices, shards(): lax.all_to_all(expert_rows, 'exp', split_axis=1, concat_axis=0, tiled=True)  47.2 us
    reduce_scatter x1, waiting for transfers between devices, shards(): lax.psum_scatter(lax.dot_general(slope, full_head, (((1,), (1,)), ((), ()...  45.4 us
    psum x1, blocking collectives, shards(): loss_sum = lax.psum(jnp.sum(own_loss), ('tok', 'exp'))  39.8 us
    all_gather x1, waiting for transfers between devices, shards(): lax.all_gather(mixed_own, 'exp', axis=0, tiled=True)  39 us
    unnamed x20, local copies, waits for them, and re-layouts  18 us
    dot_general x1, matrix products, shards(): lax.dot_general(slope, full_head, (((1,), (1,)), ((), ())), preferred_ele...  17.2 us
  transfers between devices with their start and end apart: 5, of which 5 were waited for; matrix products, arithmetic and copies ran while one was open for 0% of the time, Pallas kernels for 0%

commit v1 on v0

--- a/solution.py
+++ b/solution.py
@@ -56,7 +56,7 @@
     spread = jnp.sum(weight_slope * differ, axis=1) * mix_share * (1.0 - mix_share)
     gate_slope = spread[:, None] * differ
     router_part = jnp.dot(inputs.T, gate_slope, precision=lax.Precision.HIGHEST)
-    router_sum = lax.psum(router_part, ("tok", "exp"))
+    router_sum = lax.psum(lax.psum(router_part, "exp"), "tok")
     mean_loss = loss_sum / tokens_all
     return (own_loss, router_sum, mean_loss)
 

time: 543 us -> 512 us (0.943)
  waiting for transfers between devices: 377 us -> 343 us
    psum x1 -> x2, waiting for transfers between devices: 79.5 us -> 45.5 us  [shards(): router_sum = lax.psum(lax.psum(router_part, 'exp'), 'tok')]
  transfers between devices with their start and end apart: 5 -> 6, of which waited for: 5 -> 6; matrix products, arithmetic and copies ran while one was open for 0% -> 1% of each run, Pallas kernels for 0% -> 0%
where the time goes in v1:
time: 512 us; the launch traced here: 510 us
  waiting for transfers between devices  343 us (67%)
  blocking collectives  61.9 us (12%)
  matrix products  34.9 us (7%)
  other arithmetic  28.4 us (6%)
  local copies, waits for them, and re-layouts  19.7 us (4%)
  between operations  16.3 us (3%)
  starting transfers between devices  5.75 us (1%)
    all_gather x1, waiting for transfers between devices, shards(): full_head = lax.all_gather(head, 'tok', axis=0, tiled=True)  165 us
    all_to_all x1, waiting for transfers between devices, shards(): lax.all_to_all(expert_rows, 'exp', split_axis=1, concat_axis=0, tiled=True)  47.2 us
    psum x2, waiting for transfers between devices, shards(): router_sum = lax.psum(lax.psum(router_part, 'exp'), 'tok')  45.5 us
    reduce_scatter x1, waiting for transfers between devices, shards(): lax.psum_scatter(lax.dot_general(slope, full_head, (((1,), (1,)), ((), ()...  45.4 us
    psum x1, blocking collectives, shards(): loss_sum = lax.psum(jnp.sum(own_loss), ('tok', 'exp'))  41.6 us
    all_gather x1, waiting for transfers between devices, shards(): lax.all_gather(mixed_own, 'exp', axis=0, tiled=True)  39 us
    unnamed x20, local copies, waits for them, and re-layouts  18 us
    dot_general x1, matrix products, shards(): lax.dot_general(slope, full_head, (((1,), (1,)), ((), ())), preferred_ele...  17.2 us
  transfers between devices with their start and end apart: 6, of which 6 were waited for; matrix products, arithmetic and copies ran while one was open for 1% of the time, Pallas kernels for 0%

profile of v1, /device:TPU:1, one launch (start us, length us, event | category | flops | bytes accessed | tf_op | source)
XLA Modules:
  0.0 510.0 jit_solution(3449989466106876649)
XLA Ops:
  7.2 0.0 copy-start
  7.2 8.4 %copy.16 = bf16[1,256,4096]{2,0,1:T(2,128)(2,1)} copy(bf16[1,256,4096]{2,1,0:T(8,128)(2,1)} %param.6) | data formatting | bytes 4194304 | tf_op args[0]
  15.6 0.5 broadcast.107
  16.1 13.5 %reduce.1 = bf16[256,4096]{1,0:T(8,128)(2,1)S(1)} reduce(bf16[256,1,4096]{2,1,0:T(2,128)(2,1)} %bitcast.29, bf16[]{:T(256)} %broadcast.107), dimensions={1}, to_apply=%bitcast.25.reduce_sub_computation | reduce | bytes 4194306
  29.6 0.0 copy-start.3
  29.6 0.0 copy-start.2
  29.6 2.8 reshape.110
  32.4 5.4 %all-to-all-start = ((bf16[4,2,131072]{2,1,0:T(2,128)(2,1)}), bf16[4,2,131072]{2,1,0:T(2,128)(2,1)S(1)}, u32[]{:S(2)}, u32[]{:S(2)}) async-start(bf16[4,2,131072]{2,1,0:T(2,128)(2,1)} %reshape.110), calls=%async_computation | async-start | bytes 4194304 | tf_op jit(solution)/shard_map/all_to_all | solution.py:21
  37.8 0.0 all-gather.3.cloned.1.call-start
  37.8 0.0 copy-done.3
  37.8 0.0 copy-done
  37.8 0.0 copy-done.2
  37.9 0.5 fusion.10
  38.4 47.2 %all-to-all-done = bf16[4,2,131072]{2,1,0:T(2,128)(2,1)S(1)} async-done(((bf16[4,2,131072]{2,1,0:T(2,128)(2,1)}), bf16[4,2,131072]{2,1,0:T(2,128)(2,1)S(1)}, u32[]{:S(2)}, u32[]{:S(2)}) %all-to-all-start) | async-done | bytes 2097184 | tf_op jit(solution)/shard_map/all_to_all | solution.py:21
  85.6 3.3 reshape.111
  88.9 6.0 %copy_convert_fusion = f32[1,256,4096]{2,1,0:T(8,128)S(1)} fusion(bf16[1,256,4096]{2,0,1:T(2,128)(2,1)} %bitcast.27), kind=kLoop, calls=%fused_computation.12 | loop fusion | flops 1048576 | bytes 6291456 | tf_op jit(solution)/shard_map/convert_element_type | solution.py:22
  94.9 0.0 copy-start.5
  94.9 0.0 copy-start.4
  94.9 1.4 multiply_reduce_fusion
  96.3 0.0 all-gather.3.cloned.1.call-update
  96.3 0.0 all-gather.5.cloned.1.call-start
  96.3 0.7 all-gather.5.cloned.1.call-update
  97.1 0.2 reduce-scatter.2.cloned.1.call-start
  97.3 0.0 copy-done.5
  97.3 0.6 dynamic-slice
  98.5 0.0 copy-done.4
  98.6 0.2 dynamic-update-slice
  98.8 4.0 all-reduce
  102.8 39.0 %all-gather.3.cloned.1.call-done = bf16[256,4096]{1,0:T(8,128)(2,1)} async-done(((bf16[64,4096]{1,0:T(8,128)(2,1)}), bf16[256,4096]{1,0:T(8,128)(2,1)}) %all-gather.3.cloned.1.call-update) | async-done | bytes 2097168 | tf_op jit(solution)/shard_map/all_gather | solution.py:25
  141.8 165.1 %all-gather.5.cloned.1.call-done = bf16[4096,4000]{0,1:T(8,128)(2,1)} async-done(((bf16[512,4000]{0,1:T(8,128)(2,1)}), bf16[4096,4000]{0,1:T(8,128)(2,1)}) %all-gather.5.cloned.1.call-update) | async-done | bytes 32768016 | tf_op jit(solution)/shard_map/all_gather | solution.py:29
  306.9 16.2 %fusion.19 = (f32[256]{0:T(256)S(1)}, f32[256,4000]{0,1:T(8,128)}) fusion(bf16[256,4096]{1,0:T(8,128)(2,1)} %all-gather.3.cloned.1.call-done, bf16[4096,4000]{0,1:T(8,128)(2,1)} %all-gather.5.cloned.1.call-done), kind=kOutput, calls=%fused_computation.41 | convolution fusion | flops 8389632000 | bytes 38962176 | tf_op jit(solution)/shard_map/dot_general | solution.py:30
  323.2 9.7 %pmax.7 = f32[256]{0:T(256)S(1)} all-reduce(f32[256]{0:T(256)S(1)} %get-tuple-element.15), channel_id=1, replica_groups=mesh['tok'=8,'exp'=4] {'exp'}, use_global_device_ids=true, to_apply=%region_3.4 | all-reduce | flops 256 | bytes 2048 | tf_op jit(solution)/shard_map/pmax | solution.py:36
  332.8 3.9 fusion.1
  336.7 6.6 %all-reduce.1 = (f32[256]{0:T(256)S(1)}, f32[256]{0:T(256)S(1)}) all-reduce(f32[256]{0:T(256)S(1)} %get-tuple-element.4, f32[256]{0:T(256)S(1)} %get-tuple-element.3), channel_id=1, replica_groups=mesh['tok'=8,'exp'=4] {'exp'}, use_global_device_ids=true, to_apply=%region_5.6 | all-reduce | flops 512 | bytes 4096 | tf_op jit(solution)/shard_map/psum | solution.py:37
  343.3 17.2 %convolution_convert_fusion = bf16[256,4096]{1,0:T(8,128)(2,1)} fusion(bf16[4096,4000]{0,1:T(8,128)(2,1)} %all-gather.5.cloned.1.call-done, f32[256,4000]{0,1:T(8,128)} %get-tuple-element.16, f32[256]{0:T(256)S(1)} %get-tuple-element.10, s32[256]{0:T(256)S(1)} %all-reduce, s32[4000]{0:T(1024)S(1)} %iota_add_fusion), kind=kOutput, calls=%fused_computation | convolution fusion | flops 8395800576 | bytes 38979200 | tf_op jit(solution)/shard_map/dot_general | solution.py:48
  360.5 0.0 reduce-scatter.2.cloned.1.call-update
  360.5 0.0 all-reduce.5.cloned.1.call-start
  360.6 45.4 %reduce-scatter.2.cloned.1.call-done = bf16[64,4096]{1,0:T(8,128)(2,1)} async-done(((bf16[256,4096]{1,0:T(8,128)(2,1)}), bf16[64,4096]{1,0:T(8,128)(2,1)}) %reduce-scatter.2.cloned.1.call-update) | async-done | bytes 524304 | tf_op jit(solution)/shard_map/reduce_scatter | solution.py:47
  406.0 0.0 copy-start.1
  406.0 1.7 mul.89
  407.6 0.7 copy-done.1
  408.3 2.4 fusion
  410.7 0.1 reduce_sum.70
  410.8 1.0 convolution_bitcast_fusion
  411.8 0.0 all-reduce.5.cloned.1.call-update
  411.8 0.0 all-reduce.7.cloned.1.call-start
  411.8 32.0 %all-reduce.5.cloned.1.call-done = f32[4096,4]{0,1:T(4,128)} async-done(((f32[4096,4]{0,1:T(4,128)}), f32[4096,4]{0,1:T(4,128)}) %all-reduce.5.cloned.1.call-update) | async-done | bytes 65552 | tf_op jit(solution)/shard_map/psum | solution.py:59
  443.8 0.0 all-reduce.7.cloned.1.call-update
  443.8 1.2 fusion.17
  445.0 41.6 %psum.39 = f32[]{:T(128)} all-reduce(f32[]{:T(128)} %get-tuple-element.7), channel_id=1, replica_groups=mesh['tok'=8,'exp'=4] {'tok','exp'}, use_global_device_ids=true, to_apply=%region_14.15 | all-reduce | flops 1 | bytes 8 | tf_op jit(solution)/shard_map/psum | solution.py:43
  487.3 13.6 %all-reduce.7.cloned.1.call-done = f32[4096,4]{0,1:T(4,128)} async-done(((f32[4096,4]{0,1:T(4,128)}), f32[4096,4]{0,1:T(4,128)}) %all-reduce.7.cloned.1.call-update) | async-done | bytes 65552 | tf_op jit(solution)/shard_map/psum | solution.py:59
  500.9 1.5 copy.20
  (8 shorter events, 0.1 us)
Async XLA Ops:
  7.2 30.7 %copy-start = (bf16[64,4096]{1,0:T(8,128)(2,1)S(1)}, bf16[64,4096]{1,0:T(8,128)(2,1)}, u32[]{:S(2)}) copy-start(bf16[64,4096]{1,0:T(8,128)(2,1)} %param.7) | copy-start | bytes 1572868
  29.6 8.2 %copy-start.3 = (s32[64,2]{0,1:T(2,128)S(1)}, s32[64,2]{0,1:T(2,128)}, u32[]{:S(2)}) copy-start(s32[64,2]{0,1:T(2,128)} %param.9) | copy-start | bytes 1540
  29.6 8.2 %copy-start.2 = (f32[4096,4]{0,1:T(4,128)S(1)}, f32[4096,4]{0,1:T(4,128)}, u32[]{:S(2)}) copy-start(f32[4096,4]{0,1:T(4,128)} %param.8) | copy-start | bytes 196612
  32.4 53.2 %all-to-all-start = ((bf16[4,2,131072]{2,1,0:T(2,128)(2,1)}), bf16[4,2,131072]{2,1,0:T(2,128)(2,1)S(1)}, u32[]{:S(2)}, u32[]{:S(2)}) async-start(bf16[4,2,131072]{2,1,0:T(2,128)(2,1)} %reshape.110), calls=%async_computation | async-start | bytes 4194304 | tf_op jit(solution)/shard_map/all_to_all | solution.py:21
  37.8 104.0 %all-gather.3.cloned.1.call-start = ((), (), s32[]{:S(2)}) async-start(), calls=%async_computation.2 | async-start | bytes 2621440 | tf_op jit(solution)/shard_map/all_gather | solution.py:25
  94.9 2.4 copy-start.5
  94.9 3.6 copy-start.4
  96.3 210.6 %all-gather.5.cloned.1.call-start = ((), (), s32[]{:S(2)}) async-start(), calls=%async_computation.3 | async-start | bytes 36864000 | tf_op jit(solution)/shard_map/all_gather | solution.py:29
  97.1 308.9 %reduce-scatter.2.cloned.1.call-start = ((), (), s32[]{:S(2)}) async-start(), calls=%async_computation.4 | async-start | bytes 2621440 | tf_op jit(solution)/shard_map/reduce_scatter | solution.py:47
  360.5 83.3 %all-reduce.5.cloned.1.call-start = ((), (), s32[]{:S(2)}) async-start(), calls=%async_computation.5 | async-start | bytes 131072 | tf_op jit(solution)/shard_map/psum | solution.py:59
  406.0 2.3 copy-start.1
  411.8 89.1 %all-reduce.7.cloned.1.call-start = ((), (), s32[]{:S(2)}) async-start(), calls=%async_computation.6 | async-start | bytes 131072 | tf_op jit(solution)/shard_map/psum | solution.py:59
Sparse Core Ops, SparseCore 0:
  96.4 45.3 all-gather.2
  143.6 163.2 all-gather.4
  360.7 45.2 reduce-scatter.1
  411.9 31.8 all-reduce.4
  446.7 54.1 all-reduce.6
